TPU v7x, 32 devices: a whole 2x2x4 slice. The times are simulated.
32 devices in a mesh: samp: 16 (over z, y, x), tgt: 2 (over core).
Axes of the slice: x: 2, y: 2, z: 4, core: 2. Of those that a mesh axis runs over, the one named last changes fastest.
Arguments:
- samples: bfloat16 [3072, 128], P('samp'), may hold values from -6 to 6
- omega: bfloat16 [128, 4096], replicated, may hold values from -0.5 to 0.5
- phase: float32 [4096], replicated, may hold values from -3.140625 to 3.140625
- right_side: float32 [4096, 512], P('samp', 'tgt'), may hold values from -6 to 6
Outputs:
- weights: float32 [4096, 512], P('samp', 'tgt')
All inputs are finite; a program needn't handle non-finite values.
Results may differ from a plain program's by a relative error of at most 0.011.
The roundings to bfloat16 on the way count: a program that leaves them out, or rounds other values in their place, can miss the bound.
Values may be sent and summed in bfloat16 or wider, within the bound.
A program may use at most 128 MiB of HBM per device.

v0:
```python
import math
import jax
import jax.numpy as jnp
from jax import lax
from jax.sharding import PartitionSpec as P

ITERS = 2
ridge = 1.0


def precise_dot(left_matrix, right_matrix):
    return jnp.dot(left_matrix, right_matrix, precision=lax.Precision.HIGHEST)


def spd_solve(gram_matrix, rhs_matrix):
    factor = jnp.linalg.cholesky(gram_matrix)
    return jax.scipy.linalg.cho_solve((factor, True), rhs_matrix)


def cosine_block(samples, omega, phase, first_row, row_count):
    omega_cols = lax.dynamic_slice_in_dim(omega, first_row, row_count, 1)
    phase_cols = lax.dynamic_slice_in_dim(phase, first_row, row_count, 0)
    preact = jnp.dot(samples, omega_cols, preferred_element_type=jnp.float32) + phase_cols
    return jnp.cos(preact).astype(jnp.bfloat16)


def full_gram(stacked):
    summed = lax.psum(stacked, "samp")
    return lax.all_gather(summed, "tgt", axis=2, tiled=True)


def body(samples, omega, phase, right_side):
    feat_rows, col_count = right_side.shape
    samp_count = lax.axis_size("samp")
    feat_total = omega.shape[1]
    sample_total = samples.shape[0] * samp_count
    col_offset = lax.axis_index("tgt") * col_count
    store_block = math.gcd(feat_total, 512)
    stored = jnp.concatenate(
        [
            cosine_block(samples, omega, phase, index_block * store_block, store_block)
            for index_block in range(feat_total // store_block)
        ],
        axis=1,
    )

    def columns(first_row, row_count):
        return lax.dynamic_slice_in_dim(stored, first_row, row_count, 1)

    resid_all = lax.all_gather(right_side, "tgt", axis=1, tiled=True)
    direction_all = resid_all
    weight_own = jnp.zeros_like(right_side)
    gram_rr = full_gram(precise_dot(resid_all.T, right_side)[None])[0]
    for iteration in range(ITERS):
        direction_own = lax.dynamic_slice_in_dim(direction_all, col_offset, col_count, 1)
        initial = jnp.zeros((samples.shape[0], col_count), jnp.float32)
        shard_piece = lax.all_gather(direction_own.astype(jnp.bfloat16), "samp", axis=0, tiled=True)
        piece_rows = shard_piece.shape[0]
        block_size = math.gcd(piece_rows, 512)

        def project_one_block(index_block, acc_value):
            begin_row = index_block * block_size
            sub_piece = lax.dynamic_slice_in_dim(shard_piece, begin_row, block_size, 0)
            return acc_value + jnp.dot(
                columns(begin_row, block_size), sub_piece, preferred_element_type=jnp.float32
            )

        projected = lax.fori_loop(0, piece_rows // block_size, project_one_block, initial)
        proj_bf = projected.astype(jnp.bfloat16)
        transpose_row_count = feat_rows * lax.axis_size("samp")
        transpose_block_size = math.gcd(transpose_row_count, 512)

        def transpose_one_block(index_block, result):
            begin_row = index_block * transpose_block_size
            feats_block = columns(begin_row, transpose_block_size)
            block_term = lax.dot_general(
                feats_block, proj_bf, (((0,), (0,)), ((), ())), preferred_element_type=jnp.float32
            )
            return lax.dynamic_update_slice_in_dim(result, block_term, begin_row, 0)

        zero_rows = jnp.zeros((transpose_row_count, col_count), jnp.float32)
        summed_image = lax.psum_scatter(
            lax.fori_loop(
                0, transpose_row_count // transpose_block_size, transpose_one_block, zero_rows
            ),
            "samp",
            scatter_dimension=0,
            tiled=True,
        )
        image_own = summed_image / sample_total + ridge * direction_own
        image_all = lax.all_gather(image_own, "tgt", axis=1, tiled=True)
        gram_pq = full_gram(precise_dot(direction_all.T, image_own)[None])[0]
        alpha_coef = spd_solve(gram_pq, gram_rr)
        alpha_own = lax.dynamic_slice_in_dim(alpha_coef, col_offset, col_count, 1)
        weight_own = weight_own + precise_dot(direction_all, alpha_own)
        if iteration + 1 < ITERS:
            resid_all = resid_all - precise_dot(image_all, alpha_coef)
            resid_now = lax.dynamic_slice_in_dim(resid_all, col_offset, col_count, 1)
            gram_new = full_gram(precise_dot(resid_all.T, resid_now)[None])[0]
            beta_coef = spd_solve(gram_rr, gram_new)
            direction_all = resid_all + precise_dot(direction_all, beta_coef)
            gram_rr = gram_new
    return weight_own


def solution(mesh):
    placed = (P("samp", None), P(), P(), P("samp", "tgt"))
    return jax.shard_map(
        body, mesh=mesh, in_specs=placed, out_specs=P("samp", "tgt"), check_vma=False
    )
```

profile of v0, /device:TPU:0, one launch (start us, length us, event | category | flops | bytes accessed | tf_op | source)
XLA Modules:
  0.0 1215.1 jit_solution(10789328759363507932)
XLA Ops:
  6.5 2.6 all_gather.24
  22.8 50.4 %all-gather.7.cloned.1.call-done = bf16[4096,256]{1,0:T(8,128)(2,1)} async-done(((bf16[256,256]{1,0:T(8,128)(2,1)}), bf16[4096,256]{1,0:T(8,128)(2,1)}) %all-gather.7.cloned.1.call-update) | async-done | bytes 2097168 | tf_op jit(solution)/shard_map/all_gather | solution.py:57
  73.3 9.8 while.62
  85.3 8.6 while.60
  96.3 91.8 %reduce-scatter.3.cloned.1.call-done = f32[256,256]{1,0:T(8,128)} async-done(((f32[4096,256]{1,0:T(8,128)}), f32[256,256]{1,0:T(8,128)}) %reduce-scatter.3.cloned.1.call-update) | async-done | bytes 262160 | tf_op jit(solution)/shard_map/reduce_scatter | solution.py:82
  190.6 114.9 %all-reduce.10.cloned.1.call-done = (f32[1,512,256]{1,2,0:T(8,128)}, f32[1,512,256]{1,2,0:T(8,128)}) async-done(((f32[1,512,256]{1,2,0:T(8,128)}, f32[1,512,256]{1,2,0:T(8,128)}), (f32[1,512,256]{1,2,0:T(8,128)}, f32[1,512,256]{1,2,0:T(8,128)})) %all-reduce.10.cloned.1.call-update) | async-done | bytes 1048592 | tf_op jit(solution)/shard_map/psum | solution.py:28
  307.9 7.1 all-gather.9.cloned.1.call-done
  315.0 2.6 copy.5
  320.1 11.7 cholesky.374
  332.0 9.8 custom-call.35
  344.3 11.7 cholesky.393
  356.1 10.0 custom-call.36
  367.6 11.7 cholesky.414
  380.0 9.8 custom-call.37
  391.3 11.7 cholesky.431
  408.6 12.0 while.64
  420.6 39.3 %custom-call.38 = f32[4,128,128]{1,2,0:T(8,128)S(1)} custom-call(f32[4,128,128]{2,1,0:T(8,128)S(1)} %get-tuple-element.377), custom_call_target="InvertDiagBlocksLowerTriangular" | custom-call | tf_op jit(solution)/shard_map/jit(_cho_solve)/triangular_solve | solution.py:17
  460.0 2.7 copy.7
  475.0 11.7 cholesky.446
  487.5 10.8 custom-call.39
  502.1 12.5 %cholesky.465 = f32[128,128]{1,0:T(8,128)S(1)} custom-call(f32[128,128]{1,0:T(8,128)} %cholesky.603), custom_call_target="Cholesky" | custom-call | tf_op jit(solution)/shard_map/jit(cholesky)/cholesky | solution.py:16
  515.3 10.6 custom-call.40
  529.1 12.5 %cholesky.486 = f32[128,128]{1,0:T(8,128)} custom-call(f32[128,128]{1,0:T(8,128)S(1)} %cholesky.608), custom_call_target="Cholesky" | custom-call | tf_op jit(solution)/shard_map/jit(cholesky)/cholesky | solution.py:16
  543.1 10.4 custom-call.41
  555.9 12.3 %cholesky.503 = f32[128,128]{1,0:T(8,128)} custom-call(f32[128,128]{1,0:T(8,128)S(1)} %convolution_subtract_fusion.26), custom_call_target="Cholesky" | custom-call | tf_op jit(solution)/shard_map/jit(cholesky)/cholesky | solution.py:16
  578.3 105.3 %all-reduce.6.cloned.1.call-done = f32[1,512,256]{2,1,0:T(8,128)} async-done(((f32[1,512,256]{2,1,0:T(8,128)}), f32[1,512,256]{2,1,0:T(8,128)}) %all-reduce.6.cloned.1.call-update) | async-done | bytes 524304 | tf_op jit(solution)/shard_map/psum | solution.py:28
  684.4 14.8 %while.65 = (s32[]{:T(128)}, f32[512,512]{1,0:T(8,128)}, s32[4,2]{0,1:T(2,128)S(1)}, f32[4,128,128]{2,1,0:T(8,128)}, s32[]{:T(128)}) while((s32[]{:T(128)}, f32[512,512]{1,0:T(8,128)}, s32[4,2]{0,1:T(2,128)S(1)}, f32[4,128,128]{2,1,0:T(8,128)}, s32[]{:T(128)}) %tuple.227), condition=%wide.while_cond.clone, body=%wide.while_body.clone.sunk | while | flops 2 | bytes 132705 | solution.py:17
  685.5 2.9 bitcast_dynamic-update-slice_fusion.7
  689.1 3.0 bitcast_dynamic-update-slice_fusion.7
  692.7 2.9 bitcast_dynamic-update-slice_fusion.7
  696.3 2.9 bitcast_dynamic-update-slice_fusion.7
  699.2 40.8 %custom-call.42 = f32[4,128,128]{1,2,0:T(8,128)} custom-call(f32[4,128,128]{2,1,0:T(8,128)} %get-tuple-element.378), custom_call_target="InvertDiagBlocksLowerTriangular" | custom-call | tf_op jit(solution)/shard_map/jit(_cho_solve)/triangular_solve | solution.py:17
  752.9 59.5 %all-gather.15.cloned.1.call-done = bf16[4096,256]{1,0:T(8,128)(2,1)} async-done(((bf16[256,256]{1,0:T(8,128)(2,1)}), bf16[4096,256]{1,0:T(8,128)(2,1)}) %all-gather.15.cloned.1.call-update) | async-done | bytes 2097168 | tf_op jit(solution)/shard_map/all_gather | solution.py:57
  812.4 9.8 while.63
  824.4 8.6 while.61
  833.1 94.1 %reduce-scatter.5.cloned.1.call-done = f32[256,256]{1,0:T(8,128)} async-done(((f32[4096,256]{1,0:T(8,128)}), f32[256,256]{1,0:T(8,128)}) %reduce-scatter.5.cloned.1.call-update) | async-done | bytes 262160 | tf_op jit(solution)/shard_map/reduce_scatter | solution.py:82
  929.9 111.0 %all-reduce.8.cloned.1.call-done = f32[1,512,256]{1,2,0:T(8,128)} async-done(((f32[1,512,256]{1,2,0:T(8,128)}), f32[1,512,256]{1,2,0:T(8,128)}) %all-reduce.8.cloned.1.call-update) | async-done | bytes 524304 | tf_op jit(solution)/shard_map/psum | solution.py:28
  1042.0 8.5 all-gather.17.cloned.1.call-done
  1050.5 2.6 copy.10
  1055.6 11.7 cholesky.518
  1067.5 9.8 custom-call.43
  1079.8 11.7 cholesky.537
  1092.9 10.0 custom-call.44
  1104.4 11.7 cholesky.558
  1116.8 9.8 custom-call.45
  1128.1 11.7 cholesky.575
  1144.4 11.5 while.66
  1155.9 39.3 %custom-call.46 = f32[4,128,128]{1,2,0:T(8,128)S(1)} custom-call(f32[4,128,128]{2,1,0:T(8,128)S(1)} %get-tuple-element.379), custom_call_target="InvertDiagBlocksLowerTriangular" | custom-call | tf_op jit(solution)/shard_map/jit(_cho_solve)/triangular_solve | solution.py:17
  (276 shorter events, 173.6 us)
Async XLA Ops:
  6.5 4.2 copy-start
  6.5 6.5 copy-start.26
  6.5 66.7 %all-gather.7.cloned.1.call-start = ((), (), s32[]{:S(2)}) async-start(), calls=%async_computation.2 | async-start | bytes 2228224 | tf_op jit(solution)/shard_map/all_gather | solution.py:57
  9.9 178.2 %reduce-scatter.3.cloned.1.call-start = ((), (), s32[]{:S(2)}) async-start(), calls=%async_computation.3 | async-start | bytes 4456448 | tf_op jit(solution)/shard_map/reduce_scatter | solution.py:82
  93.9 0.9 copy-start.19
  93.9 211.5 %all-reduce.10.cloned.1.call-start = ((), (), s32[]{:S(2)}) async-start(), calls=%async_computation.12 | async-start | bytes 2097152 | tf_op jit(solution)/shard_map/psum | solution.py:28
  190.5 124.4 %all-gather.9.cloned.1.call-start = ((), (), s32[]{:S(2)}) async-start(), calls=%async_computation.4 | async-start | bytes 1572864 | tf_op jit(solution)/shard_map/all_gather | solution.py:29
  305.5 154.5 %all-gather.11.cloned.1.call-start = ((), (), s32[]{:S(2)}) async-start(), calls=%async_computation.5 | async-start | bytes 1572864 | tf_op jit(solution)/shard_map/all_gather | solution.py:29
  307.8 375.8 %all-reduce.6.cloned.1.call-start = ((), (), s32[]{:S(2)}) async-start(), calls=%async_computation.6 | async-start | bytes 1048576 | tf_op jit(solution)/shard_map/psum | solution.py:28
  315.0 2.7 copy-start.9
  319.1 1.0 copy-start.15
  459.9 7.9 copy-start.20
  460.0 2.7 copy-start.1
  462.6 2.3 copy-start.7
  468.2 3.4 copy-start.21
  471.2 1.6 copy-start.2
  471.7 2.2 copy-start.10
  472.0 2.0 copy-start.12
  474.1 1.0 copy-start.16
  500.8 0.7 copy-start.23
  528.4 0.7 copy-start.24
  568.2 7.6 copy-start.25
  570.6 0.8 copy-start.4
  573.2 166.8 %all-gather.13.cloned.1.call-start = ((), (), s32[]{:S(2)}) async-start(), calls=%async_computation.7 | async-start | bytes 1572864 | tf_op jit(solution)/shard_map/all_gather | solution.py:29
  683.6 128.7 %all-gather.15.cloned.1.call-start = ((), (), s32[]{:S(2)}) async-start(), calls=%async_computation.8 | async-start | bytes 2228224 | tf_op jit(solution)/shard_map/all_gather | solution.py:57
  699.2 44.9 %copy-start.6 = (f32[512,512]{1,0:T(8,128)S(1)}, f32[512,512]{1,0:T(8,128)}, u32[]{:S(2)}) copy-start(f32[512,512]{1,0:T(8,128)} %get-tuple-element.842) | copy-start | bytes 3145732
  740.0 5.5 copy-start.22
  749.6 1.4 copy-start.5
  752.8 174.4 %reduce-scatter.5.cloned.1.call-start = ((), (), s32[]{:S(2)}) async-start(), calls=%async_computation.9 | async-start | bytes 4456448 | tf_op jit(solution)/shard_map/reduce_scatter | solution.py:82
  833.0 207.9 %copy-start.3 = (f32[128,512]{1,0:T(8,128)S(1)}, f32[128,512]{1,0:T(8,128)}, u32[]{:S(2)}) copy-start(f32[128,512]{1,0:T(8,128)} %copy-done.2) | copy-start | bytes 786436
  833.0 207.9 %copy-start.13 = (f32[128,512]{1,0:T(8,128)S(1)}, f32[128,512]{1,0:T(8,128)}, u32[]{:S(2)}) copy-start(f32[128,512]{1,0:T(8,128)} %copy-done.12) | copy-start | bytes 786436
  833.0 207.9 %copy-start.18 = (f32[128,512]{1,0:T(8,128)S(1)}, f32[128,512]{1,0:T(8,128)}, u32[]{:S(2)}) copy-start(f32[128,512]{1,0:T(8,128)} %fusion.170) | copy-start | bytes 786436
  833.0 207.9 %all-reduce.8.cloned.1.call-start = ((), (), s32[]{:S(2)}) async-start(), calls=%async_computation.10 | async-start | bytes 1048576 | tf_op jit(solution)/shard_map/psum | solution.py:28
  929.7 120.8 %all-gather.17.cloned.1.call-start = ((), (), s32[]{:S(2)}) async-start(), calls=%async_computation.11 | async-start | bytes 1572864 | tf_op jit(solution)/shard_map/all_gather | solution.py:29
  1050.5 2.7 copy-start.11
  1054.6 1.0 copy-start.14
  1155.9 42.5 %copy-start.8 = (f32[512,512]{1,0:T(8,128)S(1)}, f32[512,512]{1,0:T(8,128)}, u32[]{:S(2)}) copy-start(f32[512,512]{1,0:T(8,128)} %get-tuple-element.844) | copy-start | bytes 3145732
  1204.9 1.4 copy-start.17
Sparse Core Ops, SparseCore 0:
  10.1 63.1 all-gather.6
  94.0 94.0 reduce-scatter.2
  193.4 111.9 all-reduce.9
  306.8 8.0 all-gather.8
  316.4 10.1 all-gather.10
  573.3 110.2 all-reduce.5
  685.2 8.0 all-gather.12
  752.9 59.3 all-gather.14
  833.1 94.0 reduce-scatter.4
  932.2 108.6 all-reduce.7
  1042.4 8.0 all-gather.16
where the time goes:
time: 1230 us; the launch traced here: 1220 us
  waiting for transfers between devices  643 us (52%)
  other arithmetic  372 us (30%)
  matrix products  111 us (9%)
  local copies, waits for them, and re-layouts  60.6 us (5%)
  between operations  22.3 us (2%)
    psum x3, waiting for transfers between devices, full_gram(): summed = lax.psum(stacked, 'samp')  331 us
    another operation x43, other arithmetic, spd_solve(): factor = jnp.linalg.cholesky(gram_matrix)  243 us
    reduce_scatter x2, waiting for transfers between devices, body(): lax.psum_scatter(lax.fori_loop(0, transpose_row_count // transpose_block_...  186 us
    another operation x8, other arithmetic, spd_solve(): return jax.scipy.linalg.cho_solve((factor, True), rhs_matrix)  124 us
    all_gather x2, waiting for transfers between devices, body(): lax.all_gather(direction_own.astype(jnp.bfloat16), 'samp', axis=0, tiled=...  110 us
    another operation x40, local copies, waits for them, and re-layouts, spd_solve(): return jax.scipy.linalg.cho_solve((factor, True), rhs_matrix)  38.5 us
    another operation x42, matrix products, spd_solve(): return jax.scipy.linalg.cho_solve((factor, True), rhs_matrix)  31.8 us
  transfers between devices with their start and end apart: 11, of which 9 were waited for; matrix products, arithmetic and copies ran while one was open for 18% of the time, Pallas kernels for 0%

commit v1 on v0

--- a/solution.py
+++ b/solution.py
@@ -3,9 +3,17 @@
 import jax.numpy as jnp
 from jax import lax
 from jax.sharding import PartitionSpec as P
+from jax.lax import axis_index, axis_size, ppermute
 
 ITERS = 2
 ridge = 1.0
+
+
+def update_the_column(z, pos_dim):
+    w_next = list(z.shape[1:])
+    w_next[pos_dim] *= z.shape[0]
+    a_next = jnp.moveaxis(z, 0, pos_dim).reshape(w_next)
+    return a_next
 
 
 def precise_dot(left_matrix, right_matrix):
@@ -54,7 +62,30 @@
     for iteration in range(ITERS):
         direction_own = lax.dynamic_slice_in_dim(direction_all, col_offset, col_count, 1)
         initial = jnp.zeros((samples.shape[0], col_count), jnp.float32)
-        shard_piece = lax.all_gather(direction_own.astype(jnp.bfloat16), "samp", axis=0, tiled=True)
+
+        def _name_arrays(vector, ax_name, dimension_no):
+            shares = axis_size(ax_name)
+            views = [(w, (w + 1) % shares) for w in range(shares)]
+            line_up = [(b, h) for h, b in views]
+            formed, response = ([], [])
+            p = 0
+            while p < shares - 1:
+                if p % 2 == 0:
+                    formed.append(
+                        ppermute(formed[-1] if formed else vector, axis_name=ax_name, perm=views)
+                    )
+                else:
+                    response.append(
+                        ppermute(response[-1] if response else vector, ax_name, perm=line_up)
+                    )
+                p = p + 1
+            shaped = jnp.stack([*formed[::-1], vector, *response])
+            row_out = axis_index(ax_name) - len(formed)
+            shaped = shaped[(jnp.arange(shares) - row_out) % shares]
+            x_next = update_the_column(shaped, dimension_no)
+            return x_next
+
+        shard_piece = _name_arrays(direction_own.astype(jnp.bfloat16), "samp", 0)
         piece_rows = shard_piece.shape[0]
         block_size = math.gcd(piece_rows, 512)
 

time: 1230 us -> 1290 us (1.049)
  starting transfers between devices: 0.93 us -> 85.8 us
  waiting for transfers between devices: 643 us -> 567 us
  local copies, waits for them, and re-layouts: 60.6 us -> 99.8 us
    all_gather x2 -> x0, waiting for transfers between devices: 110 us -> none  [body(): lax.all_gather(direction_own.astype(jnp.bfloat16), 'samp', axis=0, tiled=...]
    ppermute x0 -> x30, starting transfers between devices: none -> 85.3 us  [the longest x14 80.5 us: _name_arrays(): ppermute(response[-1] if response else vector, ax_name, perm=line_up)]
    ppermute x0 -> x30, waiting for transfers between devices: none -> 39.6 us  [the longest x16 36.5 us: _name_arrays(): ppermute(formed[-1] if formed else vector, axis_name=ax_name, perm=views)]
    unnamed x54 -> x108, local copies, waits for them, and re-layouts: 5.72 us -> 38.1 us
  transfers between devices with their start and end apart: 11 -> 39, of which waited for: 9 -> 26; matrix products, arithmetic and copies ran while one was open for 18% -> 20% of each run, Pallas kernels for 0% -> 0%
where the time goes in v1:
time: 1290 us; the launch traced here: 1280 us
  waiting for transfers between devices  567 us (44%)
  other arithmetic  380 us (29%)
  matrix products  117 us (9%)
  local copies, waits for them, and re-layouts  99.8 us (8%)
  starting transfers between devices  85.8 us (7%)
  between operations  22.4 us (2%)
    psum x3, waiting for transfers between devices, full_gram(): summed = lax.psum(stacked, 'samp')  331 us
    another operation x43, other arithmetic, spd_solve(): factor = jnp.linalg.cholesky(gram_matrix)  252 us
    reduce_scatter x2, waiting for transfers between devices, body(): lax.psum_scatter(lax.fori_loop(0, transpose_row_count // transpose_block_...  180 us
    another operation x8, other arithmetic, spd_solve(): return jax.scipy.linalg.cho_solve((factor, True), rhs_matrix)  124 us
    ppermute x14, starting transfers between devices, _name_arrays(): ppermute(response[-1] if response else vector, ax_name, perm=line_up)  80.5 us
    unnamed x108, local copies, waits for them, and re-layouts  38.1 us
    another operation x40, local copies, waits for them, and re-layouts, spd_solve(): return jax.scipy.linalg.cho_solve((factor, True), rhs_matrix)  38 us
    ppermute x16, waiting for transfers between devices, _name_arrays(): ppermute(formed[-1] if formed else vector, axis_name=ax_name, perm=views)  36.5 us
  transfers between devices with their start and end apart: 39, of which 26 were waited for; matrix products, arithmetic and copies ran while one was open for 20% of the time, Pallas kernels for 0%

profile of v1, /device:TPU:0, one launch (start us, length us, event | category | flops | bytes accessed | tf_op | source)
XLA Modules:
  0.0 1278.3 jit_solution(14177337651745592348)
XLA Ops:
  23.9 6.5 collective-permute-done.1
  50.0 5.7 collective-permute-start.11
  58.7 5.7 collective-permute-start.12
  75.8 6.2 collective-permute-start.14
  101.3 9.8 while.62
  113.4 8.6 while.60
  124.4 88.9 %reduce-scatter.3.cloned.1.call-done = f32[256,256]{1,0:T(8,128)} async-done(((f32[4096,256]{1,0:T(8,128)}), f32[256,256]{1,0:T(8,128)}) %reduce-scatter.3.cloned.1.call-update) | async-done | bytes 262160 | tf_op jit(solution)/shard_map/reduce_scatter | solution.py:113
  215.8 114.8 %all-reduce.10.cloned.1.call-done = (f32[1,512,256]{1,2,0:T(8,128)}, f32[1,512,256]{1,2,0:T(8,128)}) async-done(((f32[1,512,256]{1,2,0:T(8,128)}, f32[1,512,256]{1,2,0:T(8,128)}), (f32[1,512,256]{1,2,0:T(8,128)}, f32[1,512,256]{1,2,0:T(8,128)})) %all-reduce.10.cloned.1.call-update) | async-done | bytes 1048592 | tf_op jit(solution)/shard_map/psum | solution.py:36
  333.1 7.2 all-gather.5.cloned.1.call-done
  345.4 11.7 cholesky.374
  357.2 9.8 custom-call.35
  369.6 11.7 cholesky.393
  381.3 18.5 %custom-call.36 = f32[1,128,128]{1,2,0:T(8,128)S(1)} custom-call(f32[1,128,128]{2,1,0:T(8,128)S(1)} %get-tuple-element.470), custom_call_target="InvertDiagBlocksLowerTriangular" | custom-call | tf_op jit(solution)/shard_map/jit(cholesky)/cholesky | solution.py:24
  401.4 11.7 cholesky.414
  413.8 9.8 custom-call.37
  425.1 11.7 cholesky.431
  442.3 11.5 while.64
  453.7 39.3 %custom-call.38 = f32[4,128,128]{1,2,0:T(8,128)S(1)} custom-call(f32[4,128,128]{2,1,0:T(8,128)S(1)} %get-tuple-element.377), custom_call_target="InvertDiagBlocksLowerTriangular" | custom-call | tf_op jit(solution)/shard_map/jit(_cho_solve)/triangular_solve | solution.py:25
  508.2 11.7 cholesky.446
  520.7 10.8 custom-call.39
  535.3 12.5 cholesky.465
  548.5 10.6 custom-call.40
  562.3 12.5 cholesky.486
  576.3 10.4 custom-call.41
  589.0 12.3 cholesky.503
  611.4 105.4 %all-reduce.6.cloned.1.call-done = f32[1,512,256]{2,1,0:T(8,128)} async-done(((f32[1,512,256]{2,1,0:T(8,128)}), f32[1,512,256]{2,1,0:T(8,128)}) %all-reduce.6.cloned.1.call-update) | async-done | bytes 524304 | tf_op jit(solution)/shard_map/psum | solution.py:36
  717.6 14.3 %while.65 = (s32[]{:T(128)}, f32[512,512]{1,0:T(8,128)}, s32[4,2]{0,1:T(2,128)S(1)}, f32[4,128,128]{2,1,0:T(8,128)}, s32[]{:T(128)}) while((s32[]{:T(128)}, f32[512,512]{1,0:T(8,128)}, s32[4,2]{0,1:T(2,128)S(1)}, f32[4,128,128]{2,1,0:T(8,128)}, s32[]{:T(128)}) %tuple.225), condition=%wide.while_cond.clone, body=%wide.while_body.clone.sunk | while | flops 2 | bytes 132705 | solution.py:25
  731.9 40.8 %custom-call.42 = f32[4,128,128]{1,2,0:T(8,128)} custom-call(f32[4,128,128]{2,1,0:T(8,128)} %get-tuple-element.378), custom_call_target="InvertDiagBlocksLowerTriangular" | custom-call | tf_op jit(solution)/shard_map/jit(_cho_solve)/triangular_solve | solution.py:25
  786.4 7.2 collective-permute-done.15
  810.7 5.8 collective-permute-start.25
  819.8 6.2 collective-permute-start.26
  830.4 6.2 collective-permute-start.27
  839.1 6.3 collective-permute-start.28
  848.2 6.0 collective-permute-start.29
  877.8 9.8 while.63
  889.8 8.6 while.61
  898.5 91.2 %reduce-scatter.5.cloned.1.call-done = f32[256,256]{1,0:T(8,128)} async-done(((f32[4096,256]{1,0:T(8,128)}), f32[256,256]{1,0:T(8,128)}) %reduce-scatter.5.cloned.1.call-update) | async-done | bytes 262160 | tf_op jit(solution)/shard_map/reduce_scatter | solution.py:113
  992.4 111.1 %all-reduce.8.cloned.1.call-done = f32[1,512,256]{1,2,0:T(8,128)} async-done(((f32[1,512,256]{1,2,0:T(8,128)}), f32[1,512,256]{1,2,0:T(8,128)}) %all-reduce.8.cloned.1.call-update) | async-done | bytes 524304 | tf_op jit(solution)/shard_map/psum | solution.py:36
  1104.6 8.5 all-gather.11.cloned.1.call-done
  1118.2 11.7 cholesky.518
  1130.1 9.8 custom-call.43
  1142.4 11.7 cholesky.537
  1155.5 10.0 custom-call.44
  1167.1 11.7 cholesky.558
  1179.5 9.8 custom-call.45
  1190.7 11.7 cholesky.575
  1207.0 12.0 while.66
  1219.0 39.3 %custom-call.46 = f32[4,128,128]{1,2,0:T(8,128)S(1)} custom-call(f32[4,128,128]{2,1,0:T(8,128)S(1)} %get-tuple-element.379), custom_call_target="InvertDiagBlocksLowerTriangular" | custom-call | tf_op jit(solution)/shard_map/jit(_cho_solve)/triangular_solve | solution.py:25
  (390 shorter events, 304.0 us)
Async XLA Ops:
  6.5 206.8 %reduce-scatter.3.cloned.1.call-start = ((), (), s32[]{:S(2)}) async-start(), calls=%async_computation.2 | async-start | bytes 4456448 | tf_op jit(solution)/shard_map/reduce_scatter | solution.py:113
  9.2 12.4 collective-permute-start
  12.1 20.7 %collective-permute-start.8 = (bf16[256,256]{1,0:T(8,128)(2,1)S(1)}, bf16[256,256]{1,0:T(8,128)(2,1)S(1)}, u32[]{:S(2)}, u32[]{:S(2)}) collective-permute-start(bf16[256,256]{1,0:T(8,128)(2,1)S(1)} %dynamic-slice_convert_fusion.1), channel_id=1, source_target_pairs={{2,0},{4,2},{6,4},{8,6},{10,8},{12,10},{14,12},{16,14},{18,16},{20... | collective-permute-start | bytes 393224 | tf_op jit(solution)/shard_map/ppermute | solution.py:79
  21.6 8.9 collective-permute-start.1
  30.5 8.7 collective-permute-start.2
  32.8 8.7 collective-permute-start.9
  39.1 8.6 collective-permute-start.3
  41.4 8.6 collective-permute-start.10
  47.7 8.6 collective-permute-start.4
  50.0 8.7 collective-permute-start.11
  56.3 8.6 collective-permute-start.5
  58.7 8.8 collective-permute-start.12
  64.9 8.9 collective-permute-start.6
  67.5 8.3 collective-permute-start.13
  73.8 8.9 collective-permute-start.7
  75.8 21.2 %collective-permute-start.14 = (bf16[256,256]{1,0:T(8,128)(2,1)}, bf16[256,256]{1,0:T(8,128)(2,1)S(1)}, u32[]{:S(2)}, u32[]{:S(2)}) collective-permute-start(bf16[256,256]{1,0:T(8,128)(2,1)} %collective-permute-done.13), channel_id=1, source_target_pairs={{2,0},{4,2},{6,4},{8,6},{10,8},{12,10},{14,12},{16,14},{18,16},{20... | collective-permute-start | bytes 393224 | tf_op jit(solution)/shard_map/ppermute | solution.py:79
  122.0 208.6 %all-reduce.10.cloned.1.call-start = ((), (), s32[]{:S(2)}) async-start(), calls=%async_computation.10 | async-start | bytes 2097152 | tf_op jit(solution)/shard_map/psum | solution.py:36
  215.7 124.6 %all-gather.5.cloned.1.call-start = ((), (), s32[]{:S(2)}) async-start(), calls=%async_computation.3 | async-start | bytes 1572864 | tf_op jit(solution)/shard_map/all_gather | solution.py:37
  330.6 162.5 %all-gather.7.cloned.1.call-start = ((), (), s32[]{:S(2)}) async-start(), calls=%async_computation.4 | async-start | bytes 1572864 | tf_op jit(solution)/shard_map/all_gather | solution.py:37
  333.0 383.8 %all-reduce.6.cloned.1.call-start = ((), (), s32[]{:S(2)}) async-start(), calls=%async_computation.5 | async-start | bytes 1048576 | tf_op jit(solution)/shard_map/psum | solution.py:36
  606.4 166.4 %all-gather.9.cloned.1.call-start = ((), (), s32[]{:S(2)}) async-start(), calls=%async_computation.6 | async-start | bytes 1572864 | tf_op jit(solution)/shard_map/all_gather | solution.py:37
  716.8 272.9 %reduce-scatter.5.cloned.1.call-start = ((), (), s32[]{:S(2)}) async-start(), calls=%async_computation.7 | async-start | bytes 4456448 | tf_op jit(solution)/shard_map/reduce_scatter | solution.py:113
  731.9 44.9 %copy-start.7 = (f32[512,512]{1,0:T(8,128)S(1)}, f32[512,512]{1,0:T(8,128)}, u32[]{:S(2)}) copy-start(f32[512,512]{1,0:T(8,128)} %get-tuple-element.840) | copy-start | bytes 3145732
  784.9 8.7 collective-permute-start.15
  793.6 8.6 collective-permute-start.16
  793.6 8.6 collective-permute-start.23
  802.1 8.6 collective-permute-start.17
  802.2 8.6 collective-permute-start.24
  810.7 9.0 collective-permute-start.18
  810.7 36.8 %copy-start.26 = (bf16[256,256]{1,0:T(8,128)(2,1)}, bf16[256,256]{1,0:T(8,128)(2,1)S(1)}, u32[]{:S(2)}) copy-start(bf16[256,256]{1,0:T(8,128)(2,1)S(1)} %collective-permute-done.24) | copy-start | bytes 393220
  810.7 9.1 collective-permute-start.25
  819.7 10.0 collective-permute-start.19
  819.8 9.9 collective-permute-start.26
  829.7 9.0 collective-permute-start.20
  830.4 8.7 collective-permute-start.27
  838.7 8.8 collective-permute-start.21
  839.1 9.1 collective-permute-start.28
  847.5 8.9 collective-permute-start.22
  847.5 20.8 %copy-start.27 = (bf16[256,256]{1,0:T(8,128)(2,1)S(1)}, bf16[256,256]{1,0:T(8,128)(2,1)}, u32[]{:S(2)}) copy-start(bf16[256,256]{1,0:T(8,128)(2,1)} %copy-done.26) | copy-start | bytes 393220
  847.5 21.5 %copy-start.30 = (bf16[256,256]{1,0:T(8,128)(2,1)S(1)}, bf16[256,256]{1,0:T(8,128)(2,1)}, u32[]{:S(2)}) copy-start(bf16[256,256]{1,0:T(8,128)(2,1)} %copy-done.29) | copy-start | bytes 393220
  847.6 22.1 %copy-start.32 = (bf16[256,256]{1,0:T(8,128)(2,1)S(1)}, bf16[256,256]{1,0:T(8,128)(2,1)}, u32[]{:S(2)}) copy-start(bf16[256,256]{1,0:T(8,128)(2,1)} %copy-done.31) | copy-start | bytes 393220
  848.2 25.2 %collective-permute-start.29 = (bf16[256,256]{1,0:T(8,128)(2,1)}, bf16[256,256]{1,0:T(8,128)(2,1)S(1)}, u32[]{:S(2)}, u32[]{:S(2)}) collective-permute-start(bf16[256,256]{1,0:T(8,128)(2,1)} %collective-permute-done.28), channel_id=1, source_target_pairs={{2,0},{4,2},{6,4},{8,6},{10,8},{12,10},{14,12},{16,14},{18,16},{20... | collective-permute-start | bytes 393224 | tf_op jit(solution)/shard_map/ppermute | solution.py:79
  898.5 205.1 %copy-start.4 = (f32[128,512]{1,0:T(8,128)S(1)}, f32[128,512]{1,0:T(8,128)}, u32[]{:S(2)}) copy-start(f32[128,512]{1,0:T(8,128)} %copy-done.3) | copy-start | bytes 786436
  898.5 205.1 %copy-start.14 = (f32[128,512]{1,0:T(8,128)S(1)}, f32[128,512]{1,0:T(8,128)}, u32[]{:S(2)}) copy-start(f32[128,512]{1,0:T(8,128)} %copy-done.13) | copy-start | bytes 786436
  898.5 205.1 %copy-start.19 = (f32[128,512]{1,0:T(8,128)S(1)}, f32[128,512]{1,0:T(8,128)}, u32[]{:S(2)}) copy-start(f32[128,512]{1,0:T(8,128)} %fusion.170) | copy-start | bytes 786436
  898.5 205.0 %all-reduce.8.cloned.1.call-start = ((), (), s32[]{:S(2)}) async-start(), calls=%async_computation.8 | async-start | bytes 1048576 | tf_op jit(solution)/shard_map/psum | solution.py:36
  992.2 120.9 %all-gather.11.cloned.1.call-start = ((), (), s32[]{:S(2)}) async-start(), calls=%async_computation.9 | async-start | bytes 1572864 | tf_op jit(solution)/shard_map/all_gather | solution.py:37
  1219.0 42.5 %copy-start.9 = (f32[512,512]{1,0:T(8,128)S(1)}, f32[512,512]{1,0:T(8,128)}, u32[]{:S(2)}) copy-start(f32[512,512]{1,0:T(8,128)} %get-tuple-element.842) | copy-start | bytes 3145732
  (30 other events, 144.6 us)
Sparse Core Ops, SparseCore 0:
  122.2 91.0 reduce-scatter.2
  218.6 111.9 all-reduce.9
  332.1 8.0 all-gather.4
  341.7 10.2 all-gather.6
  606.5 110.2 all-reduce.5
  718.2 8.0 all-gather.8
  898.6 91.0 reduce-scatter.4
  994.9 108.5 all-reduce.7
  1105.1 8.0 all-gather.10
